TPU v7x, 32 devices: a whole 2x2x4 slice. The times are simulated.
32 devices in a mesh: dap: 8 (over z, x), cplx: 4 (over y, core).
Axes of the slice: x: 2, y: 2, z: 4, core: 2. Of those that a mesh axis runs over, the one named last changes fastest.
Arguments:
- pair: bfloat16 [96, 384, 128], P('dap', 'cplx'), parts along dimension 1, may hold values from -6 to 6
- cotangent: bfloat16 [96, 384, 128], P('dap', 'cplx'), parts along dimension 1, may hold values from -6 to 6
- residue_mask: int32 [384], P('cplx'), parts along dimension 0, may hold values 0 or 1
- chain_ids: int32 [384], P('cplx'), parts along dimension 0, may hold values from 0 to 2, never falling along the last dimension, each value on 1 to 48 neighbouring positions
- chain_embed: float32 [2, 128], replicated, may hold values from -4 to 4
- out_norm_gain: float32 [128], replicated, may hold values from 0.25 to 1.75
- out_proj: bfloat16 [128, 512], replicated, may hold values from -0.5 to 0.5
- out_gate: bfloat16 [128, 128], replicated, may hold values from -0.5 to 0.5
- out_mid_gain: float32 [128], replicated, may hold values from 0.25 to 1.75
- out_final: bfloat16 [128, 128], replicated, may hold values from -0.5 to 0.5
- in_norm_gain: float32 [128], replicated, may hold values from 0.25 to 1.75
- in_proj: bfloat16 [128, 512], replicated, may hold values from -0.5 to 0.5
- in_gate: bfloat16 [128, 128], replicated, may hold values from -0.5 to 0.5
- in_mid_gain: float32 [128], replicated, may hold values from 0.25 to 1.75
- in_final: bfloat16 [128, 128], replicated, may hold values from -0.5 to 0.5
Outputs:
- pair_grad: bfloat16 [96, 384, 128], P('dap', 'cplx'), parts along dimension 1
- grad_proj: float32 [512, 512], P('cplx'), parts along dimension 0
- grad_gate: float32 [512, 128], P('cplx'), parts along dimension 0
- grad_final: float32 [512, 128], P('cplx'), parts along dimension 0
- grad_norm_gain: float32 [512], P('cplx'), parts along dimension 0
- grad_mid_gain: float32 [512], P('cplx'), parts along dimension 0
There are 4 independent parts, one for each index of `cplx`. A program takes and returns all parts, laid end to end along the dimension named above; an argument that names none is the same for every part. Nothing has to cross between parts.
Inputs may be any that keep to these rules, and one draw needn't show every extreme that they name: `chain_ids`: chain numbers never fall along the residues; each chain has at most 48 residues.
All inputs are finite; a program needn't handle non-finite values.
Results may differ from a plain program's by a relative error of at most 0.019.
Values may be sent and summed in bfloat16 or wider, within the bound.
A program may use at most 128 MiB of HBM per device.

v0:
```python
import jax
import jax.numpy as jnp
from jax import lax
from jax.sharding import PartitionSpec as P


def layer_norm(values_in, gain):
    average = jnp.mean(values_in, axis=-1, keepdims=True)
    centred = values_in - average
    variance = jnp.mean(centred * centred, axis=-1, keepdims=True)
    return centred * lax.rsqrt(variance + 1e-05) * gain


def gated_pair(projected, pair_mask, hidden_width):
    masked = pair_mask[..., None]
    left_act = (
        masked
        * jax.nn.sigmoid(projected[..., :hidden_width])
        * projected[..., hidden_width : 2 * hidden_width]
    )
    right_act = (
        masked
        * jax.nn.sigmoid(projected[..., 2 * hidden_width : 3 * hidden_width])
        * projected[..., 3 * hidden_width :]
    )
    return (left_act, right_act)


def shards(
    pair,
    cotangent,
    residue_mask,
    chain_ids,
    chain_embed,
    out_norm_gain,
    out_proj,
    out_gate,
    out_mid_gain,
    out_final,
    in_norm_gain,
    in_proj,
    in_gate,
    in_mid_gain,
    in_final,
):
    f32 = jnp.float32
    bf16 = jnp.bfloat16
    row_count = pair.shape[0]
    res_count = pair.shape[1]
    hidden_width = out_final.shape[0]
    inv_count = 1.0 / res_count
    row_start = lax.axis_index("dap") * row_count
    row_mask = lax.dynamic_slice_in_dim(residue_mask, row_start, row_count, 0)
    row_chain = lax.dynamic_slice_in_dim(chain_ids, row_start, row_count, 0)
    pair_mask = (row_mask[:, None] * residue_mask[None, :]).astype(f32)
    same_chain = row_chain[:, None] == chain_ids[None, :]
    start = pair.astype(f32) + jnp.where(same_chain[..., None], chain_embed[1], chain_embed[0])
    out_normed = layer_norm(start, out_norm_gain).astype(bf16)
    projected = jnp.dot(out_normed, out_proj, preferred_element_type=f32)
    left_act, right_act = gated_pair(projected, pair_mask, hidden_width)
    left_b = left_act.astype(bf16)
    right_b = right_act.astype(bf16)
    x_out = jnp.einsum(
        "ikc,jkc->ijc",
        left_b,
        lax.all_gather(right_b, "dap", axis=0, tiled=True),
        preferred_element_type=f32,
    )
    y_out = layer_norm(x_out, out_mid_gain).astype(bf16)
    update = jax.nn.sigmoid(jnp.dot(out_normed, out_gate, preferred_element_type=f32)) * jnp.dot(
        y_out, out_final, preferred_element_type=f32
    )
    pair_mid = (start + update).astype(bf16)
    mid_f32 = pair_mid.astype(f32)
    normed_f32, norm_back = jax.vjp(layer_norm, mid_f32, in_norm_gain)
    in_normed = normed_f32.astype(bf16)
    proj_in = jnp.dot(in_normed, in_proj, preferred_element_type=f32)
    (left_in, right_in), glu_back = jax.vjp(
        lambda proj_val: gated_pair(proj_val, pair_mask, hidden_width), proj_in
    )
    left_ib = left_in.astype(bf16)
    right_ib = right_in.astype(bf16)
    columns = lax.all_to_all(left_ib, "dap", split_axis=1, concat_axis=0, tiled=True)
    left_block = columns
    x_in = jnp.einsum(
        "kic,kjc->ijc",
        left_block,
        lax.all_gather(right_ib, "dap", axis=0, tiled=True),
        preferred_element_type=f32,
    )
    y_f32, mid_back = jax.vjp(layer_norm, x_in, in_mid_gain)
    y_in = y_f32.astype(bf16)
    logit = jnp.dot(in_normed, in_gate, preferred_element_type=f32)
    value = jnp.dot(y_in, in_final, preferred_element_type=f32)
    sigma = jax.nn.sigmoid(logit)
    upstream = cotangent.astype(f32)
    grad_value = (upstream * sigma).astype(bf16)
    grad_logit = (upstream * value * sigma * (1.0 - sigma)).astype(bf16)
    grad_final = jnp.einsum("ijc,ijd->cd", y_in, grad_value, preferred_element_type=f32) * inv_count
    grad_gate = (
        jnp.einsum("ijc,ijd->cd", in_normed, grad_logit, preferred_element_type=f32) * inv_count
    )
    grad_y = jnp.dot(grad_value, in_final.T, preferred_element_type=f32)
    grad_x, grad_mid = mid_back(grad_y)
    grad_x_b = grad_x.astype(bf16)
    shard_rows = lax.all_gather(grad_x_b, "dap", axis=0, tiled=True)
    left_block = left_ib
    grad_right = jnp.einsum("kic,ijc->kjc", left_block, shard_rows, preferred_element_type=f32)
    new_block = jnp.einsum("kjc,ijc->kic", right_ib, shard_rows, preferred_element_type=f32)
    grad_p = glu_back((new_block, grad_right))[0].astype(bf16)
    grad_proj = jnp.einsum("ijc,ijd->cd", in_normed, grad_p, preferred_element_type=f32) * inv_count
    grad_normed = jnp.dot(grad_p, in_proj.T, preferred_element_type=f32) + jnp.dot(
        grad_logit, in_gate.T, preferred_element_type=f32
    )
    grad_z, grad_norm = norm_back(grad_normed)
    pair_grad = (upstream + grad_z).astype(bf16)
    reduced = (
        lax.psum(grad_proj.astype(jnp.bfloat16), "dap").astype(jnp.float32),
        lax.psum(grad_gate.astype(jnp.bfloat16), "dap").astype(jnp.float32),
        lax.psum(grad_final.astype(jnp.bfloat16), "dap").astype(jnp.float32),
        lax.psum((grad_norm * inv_count).astype(jnp.bfloat16), "dap").astype(jnp.float32),
        lax.psum((grad_mid * inv_count).astype(jnp.bfloat16), "dap").astype(jnp.float32),
    )
    return (pair_grad, reduced[0], reduced[1], reduced[2], reduced[3], reduced[4])


def solution(mesh):
    placed = (
        P("dap", "cplx", None),
        P("dap", "cplx", None),
        P("cplx"),
        P("cplx"),
        P(),
        P(),
        P(),
        P(),
        P(),
        P(),
        P(),
        P(),
        P(),
        P(),
        P(),
    )
    return jax.shard_map(
        shards,
        mesh=mesh,
        in_specs=placed,
        out_specs=(
            P("dap", "cplx", None),
            P("cplx", None),
            P("cplx", None),
            P("cplx", None),
            P("cplx"),
            P("cplx"),
        ),
        check_vma=False,
    )
```

profile of v0, /device:TPU:0, one launch (start us, length us, event | category | flops | bytes accessed | tf_op | source)
XLA Modules:
  0.0 371.3 jit_solution(1143531026395006253)
XLA Ops:
  7.2 0.7 dynamic_slice.7
  8.0 0.7 broadcast_compare_fusion
  8.7 0.8 slice_bitcast_fusion.1
  9.5 1.4 fusion.41
  10.9 1.6 multiply_reduce_fusion.7
  12.5 0.7 dynamic_slice.6
  13.2 0.7 multiply_convert_fusion.10
  13.9 1.9 fusion.47
  15.9 1.1 fusion.28
  17.0 1.2 copy.47
  18.3 1.7 fusion.8
  19.9 51.8 %all-gather.4.cloned.1.call-done = bf16[96,96,128]{2,1,0:T(8,128)(2,1)} async-done(((bf16[12,96,128]{2,1,0:T(8,128)(2,1)}), bf16[96,96,128]{2,1,0:T(8,128)(2,1)}) %all-gather.4.cloned.1.call-update) | async-done | bytes 2359312 | tf_op jit(solution)/shard_map/all_gather | solution.py:66
  71.7 3.5 copy.46
  75.2 2.8 fusion.62
  81.5 1.4 copy-done.1
  82.9 1.1 multiply_convert_fusion.2
  84.0 0.9 copy.49
  84.9 3.5 all-to-all-start
  88.4 1.1 fusion.5
  89.5 17.3 %all-to-all-done = bf16[12,96,128]{2,0,1:T(8,128)(2,1)S(1)} async-done(((bf16[12,96,128]{2,0,1:T(8,128)(2,1)}), bf16[12,96,128]{2,0,1:T(8,128)(2,1)S(1)}, u32[]{:S(2)}, u32[]{:S(2)}) %all-to-all-start) | async-done | bytes 294944 | tf_op jit(solution)/shard_map/all_to_all | solution.py:83
  107.0 1.2 copy.53
  108.2 29.5 %all-gather.6.cloned.1.call-done = bf16[96,96,128]{2,1,0:T(8,128)(2,1)} async-done(((bf16[12,96,128]{2,1,0:T(8,128)(2,1)}), bf16[96,96,128]{2,1,0:T(8,128)(2,1)}) %all-gather.6.cloned.1.call-update) | async-done | bytes 2359312 | tf_op jit(solution)/shard_map/all_gather | solution.py:88
  137.7 3.5 copy.52
  141.3 3.0 fusion.64
  144.2 1.6 copy.54
  146.9 0.8 multiply_reduce_fusion.1
  147.7 1.5 add_convert_fusion.1
  149.4 1.2 copy.59
  150.6 1.2 copy.56
  153.5 0.9 fusion.16
  154.4 1.3 fusion.17
  155.7 44.1 %all-gather.8.cloned.1.call-done = bf16[96,96,128]{2,1,0:T(8,128)(2,1)} async-done(((bf16[12,96,128]{2,1,0:T(8,128)(2,1)}), bf16[96,96,128]{2,1,0:T(8,128)(2,1)}) %all-gather.8.cloned.1.call-update) | async-done | bytes 2359312 | tf_op jit(solution)/shard_map/all_gather | solution.py:106
  199.8 3.5 copy.55
  203.3 3.8 %fusion.66 = f32[128,96,12]{1,2,0:T(8,128)} fusion(bf16[96,96,128]{1,0,2:T(8,128)(2,1)S(1)} %copy.55, bf16[12,96,128]{1,0,2:T(8,128)(2,1)} %copy.59), kind=kOutput, calls=%fused_computation.126 | convolution fusion | flops 28311552 | bytes 3244032 | tf_op jit(solution)/shard_map/kjc,ijc->kic/dot_general | solution.py:109
  207.1 2.4 copy.60
  209.4 2.9 fusion.65
  212.4 1.5 copy.57
  213.9 2.4 bitcast_multiply_fusion.3
  217.3 1.0 fusion.13
  218.9 0.8 multiply_reduce_fusion.2
  220.8 1.5 fusion.19
  222.3 66.6 %all-reduce.10.cloned.1.call-done = (bf16[128,128]{1,0:T(8,128)(2,1)}, bf16[128,128]{1,0:T(8,128)(2,1)}, bf16[128]{0:T(256)(128)(2,1)}, bf16[128]{0:T(256)(128)(2,1)}) async-done(((bf16[128,128]{1,0:T(8,128)(2,1)}, bf16[128,128]{1,0:T(8,128)(2,1)}, bf16[128]{0:T(256)(128)(2,1)}, bf16[128]{0:T(256)(128)(2,1)}), (bf16[128,128]{1,0:T(8,128)(2,1)}, bf16[128,128]{1,0:T(8,128)(2,1)}, bf16[128]{0:T(256)(128)(2,1)}, ...) | async-done | bytes 66064 | tf_op jit(solution)/shard_map/psum | solution.py:119
  288.9 1.4 convert_element_type.109
  290.3 1.4 convert_element_type.111
  291.7 1.1 convert_element_type.113
  292.8 1.1 convert_element_type.115
  293.9 69.3 %all-reduce.8.cloned.1.call-done = bf16[128,512]{1,0:T(8,128)(2,1)} async-done(((bf16[128,512]{1,0:T(8,128)(2,1)}), bf16[128,512]{1,0:T(8,128)(2,1)}) %all-reduce.8.cloned.1.call-update) | async-done | bytes 131088 | tf_op jit(solution)/shard_map/psum | solution.py:118
  363.2 1.6 convert_element_type.107
  (87 shorter events, 9.3 us)
Async XLA Ops:
  7.2 73.9 %copy-start = (bf16[128,512]{1,0:T(8,128)(2,1)S(1)}, bf16[128,512]{1,0:T(8,128)(2,1)}, u32[]{:S(2)}) copy-start(bf16[128,512]{1,0:T(8,128)(2,1)} %param.26) | copy-start | bytes 393220
  7.2 64.5 %all-gather.4.cloned.1.call-start = ((), (), s32[]{:S(2)}) async-start(), calls=%async_computation.1 | async-start | bytes 2654208 | tf_op jit(solution)/shard_map/all_gather | solution.py:66
  15.9 2.4 copy-start.5
  15.9 2.4 copy-start.23
  15.9 2.4 copy-start.25
  17.0 120.7 %all-gather.6.cloned.1.call-start = ((), (), s32[]{:S(2)}) async-start(), calls=%async_computation.2 | async-start | bytes 2654208 | tf_op jit(solution)/shard_map/all_gather | solution.py:88
  75.2 3.1 copy-start.24
  78.0 1.0 copy-start.6
  78.0 1.2 copy-start.17
  78.0 1.2 copy-start.19
  78.1 2.6 copy-start.22
  79.8 0.8 copy-start.2
  81.1 7.4 %copy-start.14 = (bf16[12,96,128]{2,1,0:T(8,128)(2,1)}, bf16[12,96,128]{2,1,0:T(8,128)(2,1)S(1)}, u32[]{:S(2)}) copy-start(bf16[12,96,128]{2,1,0:T(8,128)(2,1)S(1)} %multiply_convert_fusion.4) | copy-start | bytes 884740
  81.5 1.4 copy-start.1
  82.9 5.5 %copy-start.20 = (bf16[128,128]{1,0:T(8,128)(2,1)S(1)}, bf16[128,128]{1,0:T(8,128)(2,1)}, u32[]{:S(2)}) copy-start(bf16[128,128]{1,0:T(8,128)(2,1)} %param.27) | copy-start | bytes 98308
  84.0 22.9 %copy-start.9 = (bf16[12,96,128]{2,1,0:T(8,128)(2,1)}, bf16[12,96,128]{2,1,0:T(8,128)(2,1)S(1)}, u32[]{:S(2)}) copy-start(bf16[12,96,128]{2,1,0:T(8,128)(2,1)S(1)} %get-tuple-element.22) | copy-start | bytes 884740
  84.9 22.0 %all-to-all-start = ((bf16[12,96,128]{2,0,1:T(8,128)(2,1)}), bf16[12,96,128]{2,0,1:T(8,128)(2,1)S(1)}, u32[]{:S(2)}, u32[]{:S(2)}) async-start(bf16[12,96,128]{2,0,1:T(8,128)(2,1)} %copy.49), calls=%async_computation | async-start | bytes 786432 | tf_op jit(solution)/shard_map/all_to_all | solution.py:83
  88.4 111.4 %all-gather.8.cloned.1.call-start = ((), (), s32[]{:S(2)}) async-start(), calls=%async_computation.3 | async-start | bytes 2654208 | tf_op jit(solution)/shard_map/all_gather | solution.py:106
  141.2 4.9 %copy-start.18 = (bf16[128,128]{1,0:T(8,128)(2,1)S(1)}, bf16[128,128]{1,0:T(8,128)(2,1)}, u32[]{:S(2)}) copy-start(bf16[128,128]{1,0:T(8,128)(2,1)} %param.29) | copy-start | bytes 98308
  141.2 4.9 %copy-start.21 = (f32[128]{0:T(128)S(1)}, f32[128]{0:T(128)}, u32[]{:S(2)}) copy-start(f32[128]{0:T(128)} %param.28) | copy-start | bytes 1540
  144.2 1.9 copy-start.4
  144.2 1.9 copy-start.7
  146.2 3.2 copy-start.11
  146.9 3.7 %copy-start.10 = (bf16[12,96,128]{2,1,0:T(8,128)(2,1)S(1)}, bf16[12,96,128]{2,1,0:T(8,128)(2,1)}, u32[]{:S(2)}) copy-start(bf16[12,96,128]{2,1,0:T(8,128)(2,1)} %copy-done.9) | copy-start | bytes 884740
  147.7 5.9 %copy-start.15 = (bf16[12,96,128]{2,1,0:T(8,128)(2,1)S(1)}, bf16[12,96,128]{2,1,0:T(8,128)(2,1)}, u32[]{:S(2)}) copy-start(bf16[12,96,128]{2,1,0:T(8,128)(2,1)} %copy-done.14) | copy-start | bytes 884740
  149.2 139.7 %all-reduce.10.cloned.1.call-start = ((), (), s32[]{:S(2)}) async-start(), calls=%async_computation.5 | async-start | bytes 133120 | tf_op jit(solution)/shard_map/psum | solution.py:119
  152.8 0.7 copy-start.12
  216.3 1.0 copy-start.16
  217.3 1.1 copy-start.3
  217.3 1.1 copy-start.13
  218.3 2.5 copy-start.8
  220.2 143.0 %all-reduce.8.cloned.1.call-start = ((), (), s32[]{:S(2)}) async-start(), calls=%async_computation.4 | async-start | bytes 262144 | tf_op jit(solution)/shard_map/psum | solution.py:118
Sparse Core Ops, SparseCore 0:
  17.1 54.5 all-gather.3
  84.1 53.5 all-gather.5
  149.3 50.4 all-gather.7
  220.3 68.4 all-reduce.9
  292.6 70.4 all-reduce.7
where the time goes:
time: 372 us; the launch traced here: 371 us
  waiting for transfers between devices  279 us (75%)
  local copies, waits for them, and re-layouts  27.9 us (8%)
  matrix products  23.6 us (6%)
  other arithmetic  22.7 us (6%)
  between operations  14.2 us (4%)
  starting transfers between devices  3.84 us (1%)
    psum x1, waiting for transfers between devices, shards(): lax.psum(grad_proj.astype(jnp.bfloat16), 'dap').astype(jnp.float32)  69.3 us
    psum x1, waiting for transfers between devices, shards(): lax.psum(grad_gate.astype(jnp.bfloat16), 'dap').astype(jnp.float32)  66.6 us
    all_gather x1, waiting for transfers between devices, shards(): lax.all_gather(right_b, 'dap', axis=0, tiled=True)  51.8 us
    all_gather x1, waiting for transfers between devices, shards(): shard_rows = lax.all_gather(grad_x_b, 'dap', axis=0, tiled=True)  44.1 us
    all_gather x1, waiting for transfers between devices, shards(): lax.all_gather(right_ib, 'dap', axis=0, tiled=True)  29.5 us
    all_to_all x1, waiting for transfers between devices, shards(): lax.all_to_all(left_ib, 'dap', split_axis=1, concat_axis=0, tiled=True)  17.3 us
  transfers between devices with their start and end apart: 6, of which 6 were waited for; matrix products, arithmetic and copies ran while one was open for 5% of the time, Pallas kernels for 0%

commit v1 on v0

--- a/solution.py
+++ b/solution.py
@@ -82,12 +82,22 @@
     right_ib = right_in.astype(bf16)
     columns = lax.all_to_all(left_ib, "dap", split_axis=1, concat_axis=0, tiled=True)
     left_block = columns
-    x_in = jnp.einsum(
-        "kic,kjc->ijc",
-        left_block,
-        lax.all_gather(right_ib, "dap", axis=0, tiled=True),
-        preferred_element_type=f32,
-    )
+    size, position, width = (lax.axis_size("dap"), lax.axis_index("dap"), right_ib.shape[0])
+    ahead = [(i, (i + 1) % size) for i in range(size)]
+    block, subtotal = (right_ib, None)
+    for lap in range(size):
+        arriving = lax.ppermute(block, "dap", ahead) if lap < size - 1 else None
+        take_in = jnp.einsum(
+            "kic,kjc->ijc",
+            lax.dynamic_slice_in_dim(
+                left_block, (position - lap) % size * width, block.shape[0], axis=0
+            ),
+            block,
+            preferred_element_type=f32,
+        )
+        subtotal = take_in if subtotal is None else subtotal + take_in
+        block = arriving
+    x_in = subtotal
     y_f32, mid_back = jax.vjp(layer_norm, x_in, in_mid_gain)
     y_in = y_f32.astype(bf16)
     logit = jnp.dot(in_normed, in_gate, preferred_element_type=f32)

time: 372 us -> 399 us (1.073)
  local copies, waits for them, and re-layouts: 27.9 us -> 50.4 us
  waiting for transfers between devices: 279 us -> 266 us
  starting transfers between devices: 3.84 us -> 15.3 us
  matrix products: 23.6 us -> 27.8 us
    all_gather x1 -> x0, waiting for transfers between devices: 29.5 us -> none  [shards(): lax.all_gather(right_ib, 'dap', axis=0, tiled=True)]
    ppermute x0 -> x7, waiting for transfers between devices: none -> 23.1 us  [shards(): arriving = lax.ppermute(block, 'dap', ahead) if lap < size - 1 else None]
    ppermute x0 -> x7, local copies, waits for them, and re-layouts: none -> 11.8 us  [shards(): arriving = lax.ppermute(block, 'dap', ahead) if lap < size - 1 else None]
    ppermute x0 -> x7, starting transfers between devices: none -> 8.91 us  [shards(): arriving = lax.ppermute(block, 'dap', ahead) if lap < size - 1 else None]
    unnamed x52 -> x88, local copies, waits for them, and re-layouts: 3.78 us -> 12.2 us
    dot_general x1 -> x8, local copies, waits for them, and re-layouts: 1.62 us -> 8.65 us  [shards(): jnp.einsum('kic,kjc->ijc', lax.dynamic_slice_in_dim(left_block, (position...]
    all_to_all x1, waiting for transfers between devices: 17.3 us -> 11.3 us  [shards(): lax.all_to_all(left_ib, 'dap', split_axis=1, concat_axis=0, tiled=True)]
    dot_general x1 -> x8, matrix products: 2.96 us -> 7.94 us  [shards(): jnp.einsum('kic,kjc->ijc', lax.dynamic_slice_in_dim(left_block, (position...]
  transfers between devices with their start and end apart: 6 -> 12, of which waited for: 6 -> 10; matrix products, arithmetic and copies ran while one was open for 5% -> 12% of each run, Pallas kernels for 0% -> 0%
where the time goes in v1:
time: 399 us; the launch traced here: 398 us
  waiting for transfers between devices  266 us (67%)
  local copies, waits for them, and re-layouts  50.4 us (13%)
  matrix products  27.8 us (7%)
  other arithmetic  23.8 us (6%)
  starting transfers between devices  15.3 us (4%)
  between operations  14.4 us (4%)
    psum x1, waiting for transfers between devices, shards(): lax.psum(grad_proj.astype(jnp.bfloat16), 'dap').astype(jnp.float32)  69.2 us
    psum x1, waiting for transfers between devices, shards(): lax.psum(grad_gate.astype(jnp.bfloat16), 'dap').astype(jnp.float32)  66.6 us
    all_gather x1, waiting for transfers between devices, shards(): lax.all_gather(right_b, 'dap', axis=0, tiled=True)  51.9 us
    all_gather x1, waiting for transfers between devices, shards(): shard_rows = lax.all_gather(grad_x_b, 'dap', axis=0, tiled=True)  43.8 us
    ppermute x7, waiting for transfers between devices, shards(): arriving = lax.ppermute(block, 'dap', ahead) if lap < size - 1 else None  23.1 us
    unnamed x88, local copies, waits for them, and re-layouts  12.2 us
    ppermute x7, local copies, waits for them, and re-layouts, shards(): arriving = lax.ppermute(block, 'dap', ahead) if lap < size - 1 else None  11.8 us
    all_to_all x1, waiting for transfers between devices, shards(): lax.all_to_all(left_ib, 'dap', split_axis=1, concat_axis=0, tiled=True)  11.3 us
  transfers between devices with their start and end apart: 12, of which 10 were waited for; matrix products, arithmetic and copies ran while one was open for 12% of the time, Pallas kernels for 0%

profile of v1, /device:TPU:0, one launch (start us, length us, event | category | flops | bytes accessed | tf_op | source)
XLA Modules:
  0.0 398.1 jit_solution(5873088333459473506)
XLA Ops:
  9.4 1.4 fusion.41
  10.9 1.6 multiply_reduce_fusion.7
  13.9 1.9 fusion.47
  18.2 1.6 fusion.8
  19.8 51.9 %all-gather.3.cloned.1.call-done = bf16[96,96,128]{2,1,0:T(8,128)(2,1)} async-done(((bf16[12,96,128]{2,1,0:T(8,128)(2,1)}), bf16[96,96,128]{2,1,0:T(8,128)(2,1)}) %all-gather.3.cloned.1.call-update) | async-done | bytes 2359312 | tf_op jit(solution)/shard_map/all_gather | solution.py:66
  71.7 3.5 copy.81
  75.2 2.8 fusion.62
  81.5 1.4 copy-done.1
  83.9 9.4 %collective-permute-done = bf16[12,96,128]{2,1,0:T(8,128)(2,1)S(1)} collective-permute-done((bf16[12,96,128]{2,1,0:T(8,128)(2,1)S(1)}, bf16[12,96,128]{2,1,0:T(8,128)(2,1)S(1)}, u32[]{:S(2)}, u32[]{:S(2)}) %collective-permute-start) | collective-permute-done | bytes 294944 | tf_op jit(solution)/shard_map/ppermute | solution.py:89
  94.2 6.0 %all-to-all-start = ((bf16[12,96,128]{2,0,1:T(8,128)(2,1)}), bf16[12,96,128]{2,0,1:T(8,128)(2,1)S(1)}, u32[]{:S(2)}, u32[]{:S(2)}) async-start(bf16[12,96,128]{2,0,1:T(8,128)(2,1)} %copy.84), calls=%async_computation | async-start | bytes 786432 | tf_op jit(solution)/shard_map/all_to_all | solution.py:83
  100.2 2.8 collective-permute-done.1
  104.2 11.3 %all-to-all-done = bf16[12,96,128]{2,0,1:T(8,128)(2,1)S(1)} async-done(((bf16[12,96,128]{2,0,1:T(8,128)(2,1)}), bf16[12,96,128]{2,0,1:T(8,128)(2,1)S(1)}, u32[]{:S(2)}, u32[]{:S(2)}) %all-to-all-start) | async-done | bytes 294944 | tf_op jit(solution)/shard_map/all_to_all | solution.py:83
  115.6 5.8 %collective-permute-start.3 = (bf16[12,96,128]{2,1,0:T(8,128)(2,1)}, bf16[12,96,128]{2,1,0:T(8,128)(2,1)}, u32[]{:S(2)}, u32[]{:S(2)}) collective-permute-start(bf16[12,96,128]{2,1,0:T(8,128)(2,1)} %collective-permute-done.2), channel_id=1, source_target_pairs={{0,4},{4,8},{8,12},{12,16},{16,20},{20,24},{24,28},{28,0},{1,5},{5... | collective-permute-start | bytes 884744 | tf_op jit(solution)/shard_map/ppermute | solution.py:89
  124.2 4.5 %collective-permute-done.3 = bf16[12,96,128]{2,1,0:T(8,128)(2,1)} collective-permute-done((bf16[12,96,128]{2,1,0:T(8,128)(2,1)}, bf16[12,96,128]{2,1,0:T(8,128)(2,1)}, u32[]{:S(2)}, u32[]{:S(2)}) %collective-permute-start.3) | collective-permute-done | bytes 294944 | tf_op jit(solution)/shard_map/ppermute | solution.py:89
  128.7 2.5 collective-permute-start.4
  131.5 2.0 copy.121
  135.8 1.3 copy.122
  137.1 1.3 copy.123
  139.3 1.2 copy.126
  140.5 1.2 copy.94
  141.8 1.3 fusion.66
  143.4 2.2 copy.97
  145.6 1.5 fusion.67
  148.3 2.2 copy.100
  150.5 1.5 fusion.68
  153.1 2.2 copy.103
  155.3 2.1 collective-permute-done.5
  157.5 1.3 fusion.69
  160.0 1.4 copy.106
  162.9 4.3 %collective-permute-done.6 = bf16[12,96,128]{2,1,0:T(8,128)(2,1)} collective-permute-done((bf16[12,96,128]{2,1,0:T(8,128)(2,1)}, bf16[12,96,128]{2,1,0:T(8,128)(2,1)}, u32[]{:S(2)}, u32[]{:S(2)}) %collective-permute-start.6) | collective-permute-done | bytes 294944 | tf_op jit(solution)/shard_map/ppermute | solution.py:89
  167.2 2.2 copy.109
  169.4 1.5 fusion.71
  172.1 2.1 bitcast_reduce_fusion
  175.8 1.4 add_convert_fusion.1
  181.3 1.3 fusion.17
  182.6 43.8 %all-gather.5.cloned.1.call-done = bf16[96,96,128]{2,1,0:T(8,128)(2,1)} async-done(((bf16[12,96,128]{2,1,0:T(8,128)(2,1)}), bf16[96,96,128]{2,1,0:T(8,128)(2,1)}) %all-gather.5.cloned.1.call-update) | async-done | bytes 2359312 | tf_op jit(solution)/shard_map/all_gather | solution.py:116
  226.4 3.5 copy.111
  230.0 3.8 fusion.73
  233.7 2.4 copy.116
  236.1 3.0 fusion.72
  239.1 1.5 copy.113
  240.6 2.4 bitcast_multiply_fusion.3
  247.5 1.5 fusion.19
  249.0 66.6 %all-reduce.10.cloned.1.call-done = (bf16[128,128]{1,0:T(8,128)(2,1)}, bf16[128,128]{1,0:T(8,128)(2,1)}, bf16[128]{0:T(256)(128)(2,1)}, bf16[128]{0:T(256)(128)(2,1)}) async-done(((bf16[128,128]{1,0:T(8,128)(2,1)}, bf16[128,128]{1,0:T(8,128)(2,1)}, bf16[128]{0:T(256)(128)(2,1)}, bf16[128]{0:T(256)(128)(2,1)}), (bf16[128,128]{1,0:T(8,128)(2,1)}, bf16[128,128]{1,0:T(8,128)(2,1)}, bf16[128]{0:T(256)(128)(2,1)}, ...) | async-done | bytes 66064 | tf_op jit(solution)/shard_map/psum | solution.py:129
  315.6 1.4 convert_element_type.109
  317.0 1.4 convert_element_type.111
  320.7 69.2 %all-reduce.8.cloned.1.call-done = bf16[128,512]{1,0:T(8,128)(2,1)} async-done(((bf16[128,512]{1,0:T(8,128)(2,1)}), bf16[128,512]{1,0:T(8,128)(2,1)}) %all-reduce.8.cloned.1.call-update) | async-done | bytes 131088 | tf_op jit(solution)/shard_map/psum | solution.py:128
  389.9 1.6 convert_element_type.107
  (154 shorter events, 37.8 us)
Async XLA Ops:
  7.2 73.9 %copy-start = (bf16[128,512]{1,0:T(8,128)(2,1)S(1)}, bf16[128,512]{1,0:T(8,128)(2,1)}, u32[]{:S(2)}) copy-start(bf16[128,512]{1,0:T(8,128)(2,1)} %param.26) | copy-start | bytes 393220
  7.2 64.5 %all-gather.3.cloned.1.call-start = ((), (), s32[]{:S(2)}) async-start(), calls=%async_computation.1 | async-start | bytes 2654208 | tf_op jit(solution)/shard_map/all_gather | solution.py:66
  13.9 67.6 %copy-start.26 = (f32[12,96]{1,0:T(8,128)}, f32[12,96]{1,0:T(8,128)S(1)}, u32[]{:S(2)}) copy-start(f32[12,96]{1,0:T(8,128)S(1)} %multiply_convert_fusion.10) | copy-start | bytes 13828
  15.9 2.3 copy-start.4
  15.9 2.3 copy-start.37
  15.9 2.3 copy-start.39
  75.2 3.1 copy-start.38
  78.0 1.2 copy-start.20
  78.0 1.2 copy-start.30
  78.1 2.6 copy-start.35
  80.3 3.0 copy-start.28
  81.1 22.4 %copy-start.13 = (bf16[12,96,128]{2,1,0:T(8,128)(2,1)}, bf16[12,96,128]{2,1,0:T(8,128)(2,1)S(1)}, u32[]{:S(2)}) copy-start(bf16[12,96,128]{2,1,0:T(8,128)(2,1)S(1)} %multiply_convert_fusion.4) | copy-start | bytes 884740
  81.5 1.4 copy-start.1
  82.9 20.5 %copy-start.31 = (bf16[128,128]{1,0:T(8,128)(2,1)S(1)}, bf16[128,128]{1,0:T(8,128)(2,1)}, u32[]{:S(2)}) copy-start(bf16[128,128]{1,0:T(8,128)(2,1)} %param.27) | copy-start | bytes 98308
  83.3 10.0 %copy-start.9 = (bf16[12,96,128]{2,1,0:T(8,128)(2,1)}, bf16[12,96,128]{2,1,0:T(8,128)(2,1)S(1)}, u32[]{:S(2)}) copy-start(bf16[12,96,128]{2,1,0:T(8,128)(2,1)S(1)} %get-tuple-element.24) | copy-start | bytes 884740
  83.3 10.0 %collective-permute-start = (bf16[12,96,128]{2,1,0:T(8,128)(2,1)S(1)}, bf16[12,96,128]{2,1,0:T(8,128)(2,1)S(1)}, u32[]{:S(2)}, u32[]{:S(2)}) collective-permute-start(bf16[12,96,128]{2,1,0:T(8,128)(2,1)S(1)} %get-tuple-element.25), channel_id=1, source_target_pairs={{0,4},{4,8},{8,12},{12,16},{16,20},{20,24},{24,28},{28,0},{1,5},{5... | collective-permute-start | bytes 884744 | tf_op jit(solution)/shard_map/ppermute | solution.py:89
  93.3 9.7 %collective-permute-start.1 = (bf16[12,96,128]{2,1,0:T(8,128)(2,1)S(1)}, bf16[12,96,128]{2,1,0:T(8,128)(2,1)S(1)}, u32[]{:S(2)}, u32[]{:S(2)}) collective-permute-start(bf16[12,96,128]{2,1,0:T(8,128)(2,1)S(1)} %collective-permute-done), channel_id=1, source_target_pairs={{0,4},{4,8},{8,12},{12,16},{16,20},{20,24},{24,28},{28,0},{1,5},{5... | collective-permute-start | bytes 884744 | tf_op jit(solution)/shard_map/ppermute | solution.py:89
  94.2 21.3 %all-to-all-start = ((bf16[12,96,128]{2,0,1:T(8,128)(2,1)}), bf16[12,96,128]{2,0,1:T(8,128)(2,1)S(1)}, u32[]{:S(2)}, u32[]{:S(2)}) async-start(bf16[12,96,128]{2,0,1:T(8,128)(2,1)} %copy.84), calls=%async_computation | async-start | bytes 786432 | tf_op jit(solution)/shard_map/all_to_all | solution.py:83
  100.2 126.3 %all-gather.5.cloned.1.call-start = ((), (), s32[]{:S(2)}) async-start(), calls=%async_computation.2 | async-start | bytes 2654208 | tf_op jit(solution)/shard_map/all_gather | solution.py:116
  103.0 12.5 %copy-start.21 = (bf16[12,96,128]{2,1,0:T(8,128)(2,1)}, bf16[12,96,128]{2,1,0:T(8,128)(2,1)S(1)}, u32[]{:S(2)}) copy-start(bf16[12,96,128]{2,1,0:T(8,128)(2,1)S(1)} %collective-permute-done.1) | copy-start | bytes 884740
  103.0 12.6 %collective-permute-start.2 = (bf16[12,96,128]{2,1,0:T(8,128)(2,1)S(1)}, bf16[12,96,128]{2,1,0:T(8,128)(2,1)}, u32[]{:S(2)}, u32[]{:S(2)}) collective-permute-start(bf16[12,96,128]{2,1,0:T(8,128)(2,1)S(1)} %collective-permute-done.1), channel_id=1, source_target_pairs={{0,4},{4,8},{8,12},{12,16},{16,20},{20,24},{24,28},{28,0},{1,5},{5... | collective-permute-start | bytes 884744 | tf_op jit(solution)/shard_map/ppermute | solution.py:89
  103.4 27.7 %copy-start.8 = (bf16[12,96,128]{1,0,2:T(8,128)(2,1)}, bf16[12,96,128]{1,0,2:T(8,128)(2,1)S(1)}, u32[]{:S(2)}) copy-start(bf16[12,96,128]{1,0,2:T(8,128)(2,1)S(1)} %copy.88) | copy-start | bytes 884740
  115.6 13.1 %collective-permute-start.3 = (bf16[12,96,128]{2,1,0:T(8,128)(2,1)}, bf16[12,96,128]{2,1,0:T(8,128)(2,1)}, u32[]{:S(2)}, u32[]{:S(2)}) collective-permute-start(bf16[12,96,128]{2,1,0:T(8,128)(2,1)} %collective-permute-done.2), channel_id=1, source_target_pairs={{0,4},{4,8},{8,12},{12,16},{16,20},{20,24},{24,28},{28,0},{1,5},{5... | collective-permute-start | bytes 884744 | tf_op jit(solution)/shard_map/ppermute | solution.py:89
  123.9 7.3 %copy-start.19 = (bf16[12,12,128]{0,1,2:T(8,128)(2,1)S(1)}, bf16[12,12,128]{0,1,2:T(8,128)(2,1)}, u32[]{:S(2)}) copy-start(bf16[12,12,128]{0,1,2:T(8,128)(2,1)} %copy.119) | copy-start | bytes 110596
  128.7 17.0 %collective-permute-start.4 = (bf16[12,96,128]{2,1,0:T(8,128)(2,1)}, bf16[12,96,128]{2,1,0:T(8,128)(2,1)}, u32[]{:S(2)}, u32[]{:S(2)}) collective-permute-start(bf16[12,96,128]{2,1,0:T(8,128)(2,1)} %collective-permute-done.3), channel_id=1, source_target_pairs={{0,4},{4,8},{8,12},{12,16},{16,20},{20,24},{24,28},{28,0},{1,5},{5... | collective-permute-start | bytes 884744 | tf_op jit(solution)/shard_map/ppermute | solution.py:89
  131.4 4.4 %copy-start.23 = (bf16[12,12,128]{2,0,1:T(8,128)(2,1)S(1)}, bf16[12,12,128]{2,0,1:T(8,128)(2,1)}, u32[]{:S(2)}) copy-start(bf16[12,12,128]{2,0,1:T(8,128)(2,1)} %get-tuple-element.32) | copy-start | bytes 110596
  134.6 5.9 %copy-start.22 = (bf16[12,96,128]{2,1,0:T(8,128)(2,1)S(1)}, bf16[12,96,128]{2,1,0:T(8,128)(2,1)}, u32[]{:S(2)}) copy-start(bf16[12,96,128]{2,1,0:T(8,128)(2,1)} %copy-done.21) | copy-start | bytes 884740
  135.8 5.9 %copy-start.18 = (bf16[12,12,128]{0,1,2:T(8,128)(2,1)S(1)}, bf16[12,12,128]{0,1,2:T(8,128)(2,1)}, u32[]{:S(2)}) copy-start(bf16[12,12,128]{0,1,2:T(8,128)(2,1)} %copy.121) | copy-start | bytes 110596
  145.6 11.9 %collective-permute-start.5 = (bf16[12,96,128]{2,1,0:T(8,128)(2,1)}, bf16[12,96,128]{2,1,0:T(8,128)(2,1)}, u32[]{:S(2)}, u32[]{:S(2)}) collective-permute-start(bf16[12,96,128]{2,1,0:T(8,128)(2,1)} %collective-permute-done.4), channel_id=1, source_target_pairs={{0,4},{4,8},{8,12},{12,16},{16,20},{20,24},{24,28},{28,0},{1,5},{5... | collective-permute-start | bytes 884744 | tf_op jit(solution)/shard_map/ppermute | solution.py:89
  157.5 9.7 %collective-permute-start.6 = (bf16[12,96,128]{2,1,0:T(8,128)(2,1)}, bf16[12,96,128]{2,1,0:T(8,128)(2,1)}, u32[]{:S(2)}, u32[]{:S(2)}) collective-permute-start(bf16[12,96,128]{2,1,0:T(8,128)(2,1)} %collective-permute-done.5), channel_id=1, source_target_pairs={{0,4},{4,8},{8,12},{12,16},{16,20},{20,24},{24,28},{28,0},{1,5},{5... | collective-permute-start | bytes 884744 | tf_op jit(solution)/shard_map/ppermute | solution.py:89
  162.9 9.1 %copy-start.16 = (f32[128,96,12]{0,1,2:T(8,128)S(1)}, f32[128,96,12]{0,1,2:T(8,128)}, u32[]{:S(2)}) copy-start(f32[128,96,12]{0,1,2:T(8,128)} %copy.92) | copy-start | bytes 1769476
  162.9 9.1 %copy-start.17 = (f32[128,96,12]{0,1,2:T(8,128)S(1)}, f32[128,96,12]{0,1,2:T(8,128)}, u32[]{:S(2)}) copy-start(f32[128,96,12]{0,1,2:T(8,128)} %copy.91) | copy-start | bytes 1769476
  172.1 2.2 copy-start.6
  172.1 2.2 copy-start.24
  172.1 2.2 copy-start.33
  174.2 3.3 copy-start.10
  174.9 4.3 %copy-start.25 = (bf16[128,128]{1,0:T(8,128)(2,1)S(1)}, bf16[128,128]{1,0:T(8,128)(2,1)}, u32[]{:S(2)}) copy-start(bf16[128,128]{1,0:T(8,128)(2,1)} %param.29) | copy-start | bytes 98308
  175.0 4.3 %copy-start.34 = (f32[128]{0:T(128)S(1)}, f32[128]{0:T(128)}, u32[]{:S(2)}) copy-start(f32[128]{0:T(128)} %param.28) | copy-start | bytes 1540
  175.7 4.7 %copy-start.14 = (bf16[12,96,128]{2,1,0:T(8,128)(2,1)S(1)}, bf16[12,96,128]{2,1,0:T(8,128)(2,1)}, u32[]{:S(2)}) copy-start(bf16[12,96,128]{2,1,0:T(8,128)(2,1)} %copy-done.13) | copy-start | bytes 884740
  177.2 138.4 %all-reduce.10.cloned.1.call-start = ((), (), s32[]{:S(2)}) async-start(), calls=%async_computation.4 | async-start | bytes 133120 | tf_op jit(solution)/shard_map/psum | solution.py:129
  236.1 4.5 %copy-start.27 = (f32[12,96]{1,0:T(8,128)S(1)}, f32[12,96]{1,0:T(8,128)}, u32[]{:S(2)}) copy-start(f32[12,96]{1,0:T(8,128)} %copy-done.26) | copy-start | bytes 13828
  244.0 1.1 copy-start.3
  244.0 1.1 copy-start.12
  244.0 1.1 copy-start.32
  244.0 1.1 copy-start.36
  244.0 1.6 copy-start.29
  245.0 2.5 copy-start.7
  246.9 143.0 %all-reduce.8.cloned.1.call-start = ((), (), s32[]{:S(2)}) async-start(), calls=%async_computation.3 | async-start | bytes 262144 | tf_op jit(solution)/shard_map/psum | solution.py:128
  (4 other events, 3.5 us)
Sparse Core Ops, SparseCore 0:
  17.1 54.5 all-gather.2
  177.4 49.0 all-gather.4
  247.1 68.4 all-reduce.9
  319.4 70.4 all-reduce.7
